TPU v7x, 32 devices: a whole 2x2x4 slice. The times are simulated.
32 devices in a mesh: expert: 8 (over y, x, core), replica: 4 (over z).
Axes of the slice: x: 2, y: 2, z: 4, core: 2. Of those that a mesh axis runs over, the one named last changes fastest.
Arguments:
- tokens_in: bfloat16 [8192, 2048], P(('expert', 'replica')), may hold values from -6 to 6
- cotangents: bfloat16 [8192, 8192], P(('expert', 'replica')), may hold values from -0.1796875 to 0.1796875
- left_root: bfloat16 [8, 2048, 2048], P('expert'), may hold values from -2 to 6, as said below
- right_root: bfloat16 [8, 8, 1024, 1024], P('expert', 'replica'), may hold values from -2 to 6, as said below
Outputs:
- update: bfloat16 [8, 2048, 8192], P('expert', None, 'replica')
Inputs may be any that keep to these rules, and one draw needn't show every extreme that they name: `left_root`: each matrix is symmetric. `right_root`: each block is symmetric.
All inputs are finite; a program needn't handle non-finite values.
Results may differ from a plain program's by a relative error of at most 0.0058.
Values may be sent and summed in bfloat16 or wider, within the bound.
A program may use at most 192 MiB of HBM per device.

v0:
```python
import jax
import jax.numpy as jnp
from jax import lax
from jax.sharding import PartitionSpec as P


def body(tokens_in, cotangents, left_root, right_root):
    expert_count = lax.axis_size("expert")
    replica_count = lax.axis_size("replica")
    local_experts = left_root.shape[0]
    width = left_root.shape[1]
    block_count = right_root.shape[1]
    block_size = right_root.shape[2]
    columns = cotangents.shape[1] // replica_count
    slot_count = tokens_in.shape[0] // (expert_count * local_experts)
    shaped = cotangents.reshape(1, expert_count, local_experts, slot_count, replica_count, columns)
    routed = lax.all_to_all(
        lax.all_to_all(shaped, "expert", split_axis=1, concat_axis=1, tiled=True),
        "replica",
        split_axis=4,
        concat_axis=0,
        tiled=True,
    )
    routed = routed.reshape(replica_count, expert_count, local_experts, slot_count, columns)
    tokens = tokens_in.reshape(expert_count, local_experts, slot_count, width)
    grouped = lax.all_to_all(tokens, "expert", split_axis=0, concat_axis=0, tiled=True)
    gradient = jnp.einsum(
        "rnxsd,rnxsf->xdf",
        lax.all_gather(grouped[None], "replica", axis=0, tiled=True),
        routed,
        preferred_element_type=jnp.float32,
    )
    gradient = gradient.astype(jnp.bfloat16)
    blocks = gradient.reshape(local_experts, width, block_count, block_size)
    applied = jnp.einsum("xdbk,xbkj->xdbj", blocks, right_root, preferred_element_type=jnp.float32)
    applied = applied.astype(jnp.bfloat16).reshape(local_experts, width, columns)
    update = jnp.einsum("xde,xef->xdf", left_root, applied, preferred_element_type=jnp.float32)
    return update.astype(jnp.bfloat16)


def solution(mesh):
    in_specs = (
        P(("expert", "replica"), None),
        P(("expert", "replica"), None),
        P("expert", None, None),
        P("expert", "replica", None, None),
    )
    out_specs = P("expert", None, "replica")
    return jax.shard_map(body, mesh=mesh, in_specs=in_specs, out_specs=out_specs, check_vma=False)
```

profile of v0, /device:TPU:0, one launch (start us, length us, event | category | flops | bytes accessed | tf_op | source)
XLA Modules:
  0.0 275.7 jit_solution(12691857189009747764)
XLA Ops:
  6.5 5.2 %all-to-all-start = ((bf16[8,1,32,2048]{3,2,1,0:T(8,128)(2,1)}), bf16[8,1,32,2048]{3,2,1,0:T(8,128)(2,1)S(1)}, u32[]{:S(2)}, u32[]{:S(2)}) async-start(bf16[8,1,32,2048]{3,2,1,0:T(8,128)(2,1)} %bitcast.41), calls=%async_computation | async-start | bytes 2097152 | tf_op jit(solution)/shard_map/all_to_all | solution.py:26
  11.7 7.8 %reshape.40 = bf16[1,8,1,32,4,2048]{5,4,3,1,2,0:T(4,128)(2,1)} reshape(bf16[256,8192]{1,0:T(8,128)(2,1)} %param.5) | data formatting | bytes 8388608 | tf_op jit(solution)/shard_map/reshape | solution.py:16
  19.5 6.6 %copy.13 = bf16[1,8,1,32,4,2048]{5,3,4,2,0,1:T(8,128)(2,1)} copy(bf16[1,8,1,32,4,2048]{5,4,3,1,2,0:T(4,128)(2,1)} %reshape.40) | data formatting | bytes 8388608 | tf_op jit(solution)/shard_map/reshape | solution.py:16
  26.1 1.0 all-to-all-done
  27.1 0.0 copy-start
  27.1 4.6 %all-to-all-start.1 = ((bf16[1,8,1,32,4,2048]{5,3,4,2,0,1:T(8,128)(2,1)}), bf16[1,8,1,32,4,2048]{5,3,4,2,0,1:T(8,128)(2,1)}, u32[]{:S(2)}, u32[]{:S(2)}) async-start(bf16[1,8,1,32,4,2048]{5,3,4,2,0,1:T(8,128)(2,1)} %copy.13), calls=%async_computation.1 | async-start | bytes 8388608 | tf_op jit(solution)/shard_map/all_to_all | solution.py:18
  31.7 0.0 all-gather.3.cloned.1.call-start
  31.8 0.0 copy-done
  31.8 0.7 all-gather.3.cloned.1.call-update
  32.4 48.4 %all-to-all-done.1 = bf16[1,8,1,32,4,2048]{5,3,4,2,0,1:T(8,128)(2,1)} async-done(((bf16[1,8,1,32,4,2048]{5,3,4,2,0,1:T(8,128)(2,1)}), bf16[1,8,1,32,4,2048]{5,3,4,2,0,1:T(8,128)(2,1)}, u32[]{:S(2)}, u32[]{:S(2)}) %all-to-all-start.1) | async-done | bytes 4194336 | tf_op jit(solution)/shard_map/all_to_all | solution.py:18
  80.8 4.8 %copy.14 = bf16[1,8,1,32,4,2048]{5,3,1,2,0,4:T(8,128)(2,1)} copy(bf16[1,8,1,32,4,2048]{5,3,4,2,0,1:T(8,128)(2,1)} %all-to-all-done.1) | data formatting | bytes 8388608 | tf_op jit(solution)/shard_map/all_to_all | solution.py:18
  85.6 5.0 %all-to-all-start.2 = ((bf16[1,8,1,32,4,2048]{5,3,1,2,0,4:T(8,128)(2,1)}), bf16[1,8,1,32,4,2048]{5,3,1,2,0,4:T(8,128)(2,1)}, u32[]{:S(2)}, u32[]{:S(2)}) async-start(bf16[1,8,1,32,4,2048]{5,3,1,2,0,4:T(8,128)(2,1)} %copy.14), calls=%async_computation.2 | async-start | bytes 8388608 | tf_op jit(solution)/shard_map/all_to_all | solution.py:17
  90.6 61.0 %all-gather.3.cloned.1.call-done = bf16[32,1,32,2048]{3,2,1,0:T(8,128)(2,1)} async-done(((bf16[8,1,32,2048]{3,2,1,0:T(8,128)(2,1)}), bf16[32,1,32,2048]{3,2,1,0:T(8,128)(2,1)}) %all-gather.3.cloned.1.call-update) | async-done | bytes 4194320 | tf_op jit(solution)/shard_map/all_gather | solution.py:29
  151.6 54.4 %all-to-all-done.2 = bf16[1,8,1,32,4,2048]{5,3,1,2,0,4:T(8,128)(2,1)} async-done(((bf16[1,8,1,32,4,2048]{5,3,1,2,0,4:T(8,128)(2,1)}), bf16[1,8,1,32,4,2048]{5,3,1,2,0,4:T(8,128)(2,1)}, u32[]{:S(2)}, u32[]{:S(2)}) %all-to-all-start.2) | async-done | bytes 4194336 | tf_op jit(solution)/shard_map/all_to_all | solution.py:17
  205.9 0.0 slice-start
  205.9 14.1 %bitcast_convert_fusion = bf16[2048,2048]{0,1:T(8,128)(2,1)} fusion(bf16[1,8,1,32,4,2048]{5,3,1,2,0,4:T(8,128)(2,1)} %all-to-all-done.2, bf16[4,8,32,2048]{3,2,1,0:T(8,128)(2,1)} %bitcast.44), kind=kOutput, calls=%fused_computation | convolution fusion | flops 8594128896 | bytes 16777216 | tf_op jit(solution)/shard_map/rnxsd,rnxsf->xdf/dot_general | solution.py:27
  220.1 0.0 slice-start.1
  220.1 14.8 %convolution_convert_fusion = bf16[2,2048,1024]{1,2,0:T(8,128)(2,1)} fusion(bf16[2048,2,1024]{0,2,1:T(8,128)(2,1)} %bitcast.45, bf16[1,2,1024,1024]{3,2,1,0:T(8,128)(2,1)} %param.7), kind=kOutput, calls=%fused_computation.4 | convolution fusion | flops 8594128896 | bytes 20971520 | tf_op jit(solution)/shard_map/xdbk,xbkj->xdbj/dot_general | solution.py:35
  234.9 0.0 slice-done
  234.9 0.0 slice-done.1
  234.9 21.8 %convert_bitcast_fusion = bf16[1,2048,2048]{1,2,0:T(8,128)(2,1)} fusion(bf16[2048,2048]{0,1:T(8,128)(2,1)} %bitcast.46, bf16[1,2048,2048]{2,1,0:T(8,128)(2,1)S(1)} %bitcast.43), kind=kOutput, calls=%fused_computation.3 | convolution fusion | flops 17184063488 | bytes 25165824 | tf_op jit(solution)/shard_map/xde,xef->xdf/dot_general | solution.py:37
  256.7 12.2 %copy.19 = bf16[1,2048,2048]{2,1,0:T(8,128)(2,1)} copy(bf16[1,2048,2048]{1,2,0:T(8,128)(2,1)} %convert_bitcast_fusion) | data formatting | bytes 16777216 | tf_op jit(solution)/shard_map/convert_element_type | solution.py:38
  (1 shorter events, 0.0 us)
Async XLA Ops:
  6.5 20.6 %all-to-all-start = ((bf16[8,1,32,2048]{3,2,1,0:T(8,128)(2,1)}), bf16[8,1,32,2048]{3,2,1,0:T(8,128)(2,1)S(1)}, u32[]{:S(2)}, u32[]{:S(2)}) async-start(bf16[8,1,32,2048]{3,2,1,0:T(8,128)(2,1)} %bitcast.41), calls=%async_computation | async-start | bytes 2097152 | tf_op jit(solution)/shard_map/all_to_all | solution.py:26
  27.1 4.6 %copy-start = (bf16[8,1,32,2048]{3,2,1,0:T(8,128)(2,1)}, bf16[8,1,32,2048]{3,2,1,0:T(8,128)(2,1)S(1)}, u32[]{:S(2)}) copy-start(bf16[8,1,32,2048]{3,2,1,0:T(8,128)(2,1)S(1)} %all-to-all-done) | copy-start | bytes 3145732
  27.1 53.7 %all-to-all-start.1 = ((bf16[1,8,1,32,4,2048]{5,3,4,2,0,1:T(8,128)(2,1)}), bf16[1,8,1,32,4,2048]{5,3,4,2,0,1:T(8,128)(2,1)}, u32[]{:S(2)}, u32[]{:S(2)}) async-start(bf16[1,8,1,32,4,2048]{5,3,4,2,0,1:T(8,128)(2,1)} %copy.13), calls=%async_computation.1 | async-start | bytes 8388608 | tf_op jit(solution)/shard_map/all_to_all | solution.py:18
  31.7 119.9 %all-gather.3.cloned.1.call-start = ((), (), s32[]{:S(2)}) async-start(), calls=%async_computation.3 | async-start | bytes 5242880 | tf_op jit(solution)/shard_map/all_gather | solution.py:29
  85.6 120.3 %all-to-all-start.2 = ((bf16[1,8,1,32,4,2048]{5,3,1,2,0,4:T(8,128)(2,1)}), bf16[1,8,1,32,4,2048]{5,3,1,2,0,4:T(8,128)(2,1)}, u32[]{:S(2)}, u32[]{:S(2)}) async-start(bf16[1,8,1,32,4,2048]{5,3,1,2,0,4:T(8,128)(2,1)} %copy.14), calls=%async_computation.2 | async-start | bytes 8388608 | tf_op jit(solution)/shard_map/all_to_all | solution.py:17
  205.9 28.9 %slice-start = ((s8[8388608]{0:T(1024)(128)(4,1)}), s8[4194304]{0:T(1024)(128)(4,1)S(1)}, s32[]{:S(2)}) async-start(s8[8388608]{0:T(1024)(128)(4,1)} %bitcast.42), calls=%async_computation.4 | async-start | bytes 8388608
  220.1 14.8 %slice-start.1 = ((s8[8388608]{0:T(1024)(128)(4,1)}), s8[4194304]{0:T(1024)(128)(4,1)S(1)}, s32[]{:S(2)}) async-start(s8[8388608]{0:T(1024)(128)(4,1)} %bitcast.42), calls=%async_computation.5 | async-start | bytes 8388608
Sparse Core Ops, SparseCore 0:
  34.1 117.4 all-gather.2
where the time goes:
time: 277 us; the launch traced here: 276 us
  waiting for transfers between devices  165 us (60%)
  matrix products  50.7 us (18%)
  local copies, waits for them, and re-layouts  31.4 us (11%)
  starting transfers between devices  14.8 us (5%)
  between operations  13.4 us (5%)
    all_gather x1, waiting for transfers between devices, body(): lax.all_gather(grouped[None], 'replica', axis=0, tiled=True)  61 us
    all_to_all x1, waiting for transfers between devices, body(): lax.all_to_all(lax.all_to_all(shaped, 'expert', split_axis=1, concat_axis...  54.4 us
    all_to_all x1, waiting for transfers between devices, body(): lax.all_to_all(shaped, 'expert', split_axis=1, concat_axis=1, tiled=True)  48.4 us
    dot_general x1, matrix products, body(): jnp.einsum('xde,xef->xdf', left_root, applied, preferred_element_type=jnp...  21.8 us
    dot_general x1, matrix products, body(): jnp.einsum('xdbk,xbkj->xdbj', blocks, right_root, preferred_element_type=...  14.8 us
    reshape x2, local copies, waits for them, and re-layouts, body(): cotangents.reshape(1, expert_count, local_experts, slot_count, replica_co...  14.4 us
    dot_general x1, matrix products, body(): jnp.einsum('rnxsd,rnxsf->xdf', lax.all_gather(grouped[None], 'replica', a...  14.1 us
    convert_element_type x1, local copies, waits for them, and re-layouts, body(): return update.astype(jnp.bfloat16)  12.2 us
  transfers between devices with their start and end apart: 4, of which 4 were waited for; matrix products, arithmetic and copies ran while one was open for 7% of the time, Pallas kernels for 0%

commit v1 on v0

--- a/solution.py
+++ b/solution.py
@@ -24,12 +24,42 @@
     routed = routed.reshape(replica_count, expert_count, local_experts, slot_count, columns)
     tokens = tokens_in.reshape(expert_count, local_experts, slot_count, width)
     grouped = lax.all_to_all(tokens, "expert", split_axis=0, concat_axis=0, tiled=True)
-    gradient = jnp.einsum(
+    peers, position, rows = (
+        lax.axis_size("replica"),
+        lax.axis_index("replica"),
+        grouped[None].shape[0],
+    )
+    forward = [(i, (i + 1) % peers) for i in range(peers)]
+    downward = [(i, (i - 1) % peers) for i in range(peers)]
+    middle = peers // 2
+    from_left = from_right = grouped[None]
+    subtotal = jnp.einsum(
         "rnxsd,rnxsf->xdf",
-        lax.all_gather(grouped[None], "replica", axis=0, tiled=True),
-        routed,
+        grouped[None],
+        lax.dynamic_slice_in_dim(routed, position * rows, grouped[None].shape[0], axis=0),
         preferred_element_type=jnp.float32,
     )
+    for hop in range(1, middle + 1):
+        from_left = lax.ppermute(from_left, "replica", forward)
+        if hop < peers - middle:
+            from_right = lax.ppermute(from_right, "replica", downward)
+            subtotal = subtotal + jnp.einsum(
+                "rnxsd,rnxsf->xdf",
+                from_right,
+                lax.dynamic_slice_in_dim(
+                    routed, (position + hop) % peers * rows, from_right.shape[0], axis=0
+                ),
+                preferred_element_type=jnp.float32,
+            )
+        subtotal = subtotal + jnp.einsum(
+            "rnxsd,rnxsf->xdf",
+            from_left,
+            lax.dynamic_slice_in_dim(
+                routed, (position - hop) % peers * rows, from_left.shape[0], axis=0
+            ),
+            preferred_element_type=jnp.float32,
+        )
+    gradient = subtotal
     gradient = gradient.astype(jnp.bfloat16)
     blocks = gradient.reshape(local_experts, width, block_count, block_size)
     applied = jnp.einsum("xdbk,xbkj->xdbj", blocks, right_root, preferred_element_type=jnp.float32)

time: 277 us -> 328 us (1.18)
  waiting for transfers between devices: 165 us -> 102 us
  blocking collectives: 0 us -> 54.1 us
  starting transfers between devices: 14.8 us -> 52.2 us
  matrix products: 50.7 us -> 85.7 us
  between operations: 13.4 us -> 0.03 us
    ppermute x0 -> x3, waiting for transfers between devices: none -> 91.6 us  [the longest x2 91.6 us: body(): from_left = lax.ppermute(from_left, 'replica', forward)]
    all_gather x1 -> x0, waiting for transfers between devices: 61 us -> none  [body(): lax.all_gather(grouped[None], 'replica', axis=0, tiled=True)]
    all_to_all x1, waiting for transfers between devices: 54.4 us -> 0.01 us  [body(): lax.all_to_all(lax.all_to_all(shaped, 'expert', split_axis=1, concat_axis...]
    all_to_all x0 -> x1, blocking collectives: none -> 54.1 us  [body(): lax.all_to_all(shaped, 'expert', split_axis=1, concat_axis=1, tiled=True)]
    all_to_all x1 -> x0, waiting for transfers between devices: 48.4 us -> none  [body(): lax.all_to_all(shaped, 'expert', split_axis=1, concat_axis=1, tiled=True)]
    ppermute x0 -> x3, starting transfers between devices: none -> 43.8 us  [the longest x2 42 us: body(): from_left = lax.ppermute(from_left, 'replica', forward)]
    dot_general x1 -> x4, matrix products: 14.1 us -> 49.5 us  [the longest x2 30.4 us: body(): jnp.einsum('rnxsd,rnxsf->xdf', from_left, lax.dynamic_slice_in_dim(routed...]
    all_to_all x1, waiting for transfers between devices: 1 us -> 10.5 us  [body(): lax.all_to_all(tokens, 'expert', split_axis=0, concat_axis=0, tiled=True)]
  transfers between devices with their start and end apart: 4 -> 5, of which waited for: 4 -> 2; matrix products, arithmetic and copies ran while one was open for 7% -> 10% of each run, Pallas kernels for 0% -> 0%
where the time goes in v1:
time: 328 us; the launch traced here: 324 us
  waiting for transfers between devices  102 us (31%)
  matrix products  85.7 us (26%)
  blocking collectives  54.1 us (16%)
  starting transfers between devices  52.2 us (16%)
  local copies, waits for them, and re-layouts  29.4 us (9%)
    ppermute x2, waiting for transfers between devices, body(): from_left = lax.ppermute(from_left, 'replica', forward)  91.6 us
    all_to_all x1, blocking collectives, body(): lax.all_to_all(shaped, 'expert', split_axis=1, concat_axis=1, tiled=True)  54.1 us
    ppermute x2, starting transfers between devices, body(): from_left = lax.ppermute(from_left, 'replica', forward)  42 us
    dot_general x2, matrix products, body(): jnp.einsum('rnxsd,rnxsf->xdf', from_left, lax.dynamic_slice_in_dim(routed...  30.4 us
    dot_general x1, matrix products, body(): jnp.einsum('xde,xef->xdf', left_root, applied, preferred_element_type=jnp...  21.5 us
    dot_general x1, matrix products, body(): jnp.einsum('xdbk,xbkj->xdbj', blocks, right_root, preferred_element_type=...  14.6 us
    reshape x2, local copies, waits for them, and re-layouts, body(): cotangents.reshape(1, expert_count, local_experts, slot_count, replica_co...  12.4 us
    convert_element_type x1, local copies, waits for them, and re-layouts, body(): return update.astype(jnp.bfloat16)  12.2 us
  transfers between devices with their start and end apart: 5, of which 2 were waited for; matrix products, arithmetic and copies ran while one was open for 10% of the time, Pallas kernels for 0%

profile of v1, /device:TPU:0, one launch (start us, length us, event | category | flops | bytes accessed | tf_op | source)
XLA Modules:
  0.0 323.7 jit_solution(10526201283825209460)
XLA Ops:
  0.0 7.8 %reshape.86 = bf16[1,8,1,32,4,2048]{5,4,3,1,2,0:T(4,128)(2,1)} reshape(bf16[256,8192]{1,0:T(8,128)(2,1)} %param.5) | data formatting | bytes 8388608 | tf_op jit(solution)/shard_map/reshape | solution.py:16
  7.8 4.6 %copy.13 = bf16[1,8,1,32,4,2048]{5,3,4,2,0,1:T(8,128)(2,1)S(1)} copy(bf16[1,8,1,32,4,2048]{5,4,3,1,2,0:T(4,128)(2,1)} %reshape.86) | data formatting | bytes 8388608 | tf_op jit(solution)/shard_map/reshape | solution.py:16
  12.4 54.1 %all_to_all.19 = bf16[1,8,1,32,4,2048]{5,3,4,2,0,1:T(8,128)(2,1)} all-to-all(bf16[1,8,1,32,4,2048]{5,3,4,2,0,1:T(8,128)(2,1)S(1)} %copy.13), channel_id=1, replica_groups=mesh['expert'=8,'replica'=4] {'expert'}, dimensions={1} | all-to-all | bytes 8388608 | tf_op jit(solution)/shard_map/all_to_all | solution.py:18
  66.5 3.6 %all-to-all-start.2 = ((bf16[8,1,32,2048]{3,2,1,0:T(8,128)(2,1)}), bf16[8,1,32,2048]{3,2,1,0:T(8,128)(2,1)S(1)}, u32[]{:S(2)}, u32[]{:S(2)}) async-start(bf16[8,1,32,2048]{3,2,1,0:T(8,128)(2,1)} %bitcast.1), calls=%async_computation.2 | async-start | bytes 2097152 | tf_op jit(solution)/shard_map/all_to_all | solution.py:26
  70.1 4.8 %copy.14 = bf16[1,8,1,32,4,2048]{5,3,1,2,0,4:T(8,128)(2,1)} copy(bf16[1,8,1,32,4,2048]{5,3,4,2,0,1:T(8,128)(2,1)} %all_to_all.19) | data formatting | bytes 8388608 | tf_op jit(solution)/shard_map/all_to_all | solution.py:18
  74.9 10.5 %all-to-all-done.2 = bf16[8,1,32,2048]{3,2,1,0:T(8,128)(2,1)S(1)} async-done(((bf16[8,1,32,2048]{3,2,1,0:T(8,128)(2,1)}), bf16[8,1,32,2048]{3,2,1,0:T(8,128)(2,1)S(1)}, u32[]{:S(2)}, u32[]{:S(2)}) %all-to-all-start.2) | async-done | bytes 1048608 | tf_op jit(solution)/shard_map/all_to_all | solution.py:26
  85.4 4.9 %all-to-all-start.1 = ((bf16[1,8,1,32,4,2048]{5,3,1,2,0,4:T(8,128)(2,1)}), bf16[1,8,1,32,4,2048]{5,3,1,2,0,4:T(8,128)(2,1)}, u32[]{:S(2)}, u32[]{:S(2)}) async-start(bf16[1,8,1,32,4,2048]{5,3,1,2,0,4:T(8,128)(2,1)} %copy.14), calls=%async_computation.1 | async-start | bytes 8388608 | tf_op jit(solution)/shard_map/all_to_all | solution.py:17
  90.3 2.0 collective-permute-start.1
  92.3 1.9 collective-permute-start
  94.2 91.6 %collective-permute-done.1 = bf16[1,8,1,32,2048]{4,3,1,2,0:T(8,128)(2,1)S(1)} collective-permute-done((bf16[1,8,1,32,2048]{4,3,1,2,0:T(8,128)(2,1)S(1)}, bf16[1,8,1,32,2048]{4,3,1,2,0:T(8,128)(2,1)S(1)}, u32[]{:S(2)}, u32[]{:S(2)}) %collective-permute-start.1) | collective-permute-done | bytes 1048608 | tf_op jit(solution)/shard_map/ppermute | solution.py:43
  185.8 39.9 %collective-permute-start.2 = (bf16[1,8,1,32,2048]{4,3,1,2,0:T(8,128)(2,1)S(1)}, bf16[1,8,1,32,2048]{4,3,1,2,0:T(8,128)(2,1)}, u32[]{:S(2)}, u32[]{:S(2)}) collective-permute-start(bf16[1,8,1,32,2048]{4,3,1,2,0:T(8,128)(2,1)S(1)} %collective-permute-done.1), channel_id=1, source_target_pairs={{0,1},{1,2},{2,3},{3,0},{4,5},{5,6},{6,7},{7,4},{8,9},{9,10},{10,1... | collective-permute-start | bytes 3145736 | tf_op jit(solution)/shard_map/ppermute | solution.py:43
  225.7 0.0 all-to-all-done.1
  225.7 9.4 %fusion.8 = f32[2048,2048,1]{1,0,2:T(8,128)} fusion(bf16[1,8,1,32,2048]{4,3,1,2,0:T(8,128)(2,1)S(1)} %collective-permute-done.1, bf16[1,8,1,32,4,2048]{5,3,1,2,0,4:T(8,128)(2,1)} %all-to-all-done.1, s32[]{:T(128)S(6)} %select_n.31), kind=kOutput, calls=%fused_computation.11 | convolution fusion | flops 2147483648 | bytes 18874372 | tf_op jit(solution)/shard_map/rnxsd,rnxsf->xdf/dot_general | solution.py:54
  235.1 9.3 %fusion.14 = f32[2048,2048,1]{1,0,2:T(8,128)} fusion(bf16[8,1,32,2048]{3,2,1,0:T(8,128)(2,1)S(1)} %all-to-all-done.2, bf16[1,8,1,32,4,2048]{5,3,1,2,0,4:T(8,128)(2,1)} %all-to-all-done.1, s32[]{:T(128)S(6)} %select_n.27), kind=kOutput, calls=%fused_computation.17 | convolution fusion | flops 2147483648 | bytes 18874372 | tf_op jit(solution)/shard_map/rnxsd,rnxsf->xdf/dot_general | solution.py:36
  244.4 0.0 collective-permute-done
  244.4 0.0 slice-start
  244.4 9.8 %fusion.11 = f32[2048,2048,1]{1,0,2:T(8,128)} fusion(bf16[1,8,1,32,2048]{4,3,1,2,0:T(8,128)(2,1)} %collective-permute-done, bf16[1,8,1,32,4,2048]{5,3,1,2,0,4:T(8,128)(2,1)} %all-to-all-done.1, s32[]{:T(128)S(6)} %select_n.29), kind=kOutput, calls=%fused_computation.14 | convolution fusion | flops 2147483648 | bytes 18874372 | tf_op jit(solution)/shard_map/rnxsd,rnxsf->xdf/dot_general | solution.py:46
  254.2 0.0 slice-start.1
  254.2 0.0 collective-permute-done.2
  254.2 21.1 %fusion = bf16[2048,2048]{1,0:T(8,128)(2,1)} fusion(f32[2048,2048,1]{1,0,2:T(8,128)} %fusion.8, f32[2048,2048,1]{1,0,2:T(8,128)} %fusion.11, f32[2048,2048,1]{1,0,2:T(8,128)} %fusion.14, bf16[1,8,1,32,2048]{4,3,1,2,0:T(8,128)(2,1)} %collective-permute-done.2, bf16[1,8,1,32,4,2048]{5,3,1,2,0,4:T(8,128)(2,1)} %all-to-all-done.1, s32[]{:T(128)S(6)} %select_n.33), kind=kOutput, calls=%fused_computation.1 | convolution fusion | flops 2164260864 | bytes 60817412 | tf_op jit(solution)/shard_map/rnxsd,rnxsf->xdf/dot_general | solution.py:54
  275.3 14.6 %convolution_convert_fusion = bf16[2,2048,1024]{1,2,0:T(8,128)(2,1)} fusion(bf16[2048,2,1024]{0,2,1:T(8,128)(2,1)} %bitcast.68, bf16[1,2,1024,1024]{3,2,1,0:T(8,128)(2,1)} %param.7), kind=kOutput, calls=%fused_computation.7 | convolution fusion | flops 8594128896 | bytes 20971520 | tf_op jit(solution)/shard_map/xdbk,xbkj->xdbj/dot_general | solution.py:65
  289.9 0.0 slice-done
  289.9 0.0 slice-done.1
  289.9 21.5 %convert_bitcast_fusion = bf16[1,2048,2048]{1,2,0:T(8,128)(2,1)} fusion(bf16[2048,2048]{0,1:T(8,128)(2,1)} %bitcast.69, bf16[1,2048,2048]{2,1,0:T(8,128)(2,1)S(1)} %bitcast.67), kind=kOutput, calls=%fused_computation.6 | convolution fusion | flops 17184063488 | bytes 25165824 | tf_op jit(solution)/shard_map/xde,xef->xdf/dot_general | solution.py:67
  311.5 12.2 %copy.17 = bf16[1,2048,2048]{2,1,0:T(8,128)(2,1)} copy(bf16[1,2048,2048]{1,2,0:T(8,128)(2,1)} %convert_bitcast_fusion) | data formatting | bytes 16777216 | tf_op jit(solution)/shard_map/convert_element_type | solution.py:68
  (1 shorter events, 0.0 us)
Async XLA Ops:
  66.5 18.9 %all-to-all-start.2 = ((bf16[8,1,32,2048]{3,2,1,0:T(8,128)(2,1)}), bf16[8,1,32,2048]{3,2,1,0:T(8,128)(2,1)S(1)}, u32[]{:S(2)}, u32[]{:S(2)}) async-start(bf16[8,1,32,2048]{3,2,1,0:T(8,128)(2,1)} %bitcast.1), calls=%async_computation.2 | async-start | bytes 2097152 | tf_op jit(solution)/shard_map/all_to_all | solution.py:26
  85.4 140.3 %all-to-all-start.1 = ((bf16[1,8,1,32,4,2048]{5,3,1,2,0,4:T(8,128)(2,1)}), bf16[1,8,1,32,4,2048]{5,3,1,2,0,4:T(8,128)(2,1)}, u32[]{:S(2)}, u32[]{:S(2)}) async-start(bf16[1,8,1,32,4,2048]{5,3,1,2,0,4:T(8,128)(2,1)} %copy.14), calls=%async_computation.1 | async-start | bytes 8388608 | tf_op jit(solution)/shard_map/all_to_all | solution.py:17
  90.3 95.5 %collective-permute-start.1 = (bf16[1,8,1,32,2048]{4,3,1,2,0:T(8,128)(2,1)S(1)}, bf16[1,8,1,32,2048]{4,3,1,2,0:T(8,128)(2,1)S(1)}, u32[]{:S(2)}, u32[]{:S(2)}) collective-permute-start(bf16[1,8,1,32,2048]{4,3,1,2,0:T(8,128)(2,1)S(1)} %bitcast.64), channel_id=1, source_target_pairs={{0,1},{1,2},{2,3},{3,0},{4,5},{5,6},{6,7},{7,4},{8,9},{9,10},{10,1... | collective-permute-start | bytes 3145736 | tf_op jit(solution)/shard_map/ppermute | solution.py:43
  92.3 152.1 %collective-permute-start = (bf16[1,8,1,32,2048]{4,3,1,2,0:T(8,128)(2,1)S(1)}, bf16[1,8,1,32,2048]{4,3,1,2,0:T(8,128)(2,1)}, u32[]{:S(2)}, u32[]{:S(2)}) collective-permute-start(bf16[1,8,1,32,2048]{4,3,1,2,0:T(8,128)(2,1)S(1)} %bitcast.65), channel_id=1, source_target_pairs={{0,3},{1,0},{2,1},{3,2},{4,7},{5,4},{6,5},{7,6},{8,11},{9,8},{10,9... | collective-permute-start | bytes 3145736 | tf_op jit(solution)/shard_map/ppermute | solution.py:45
  185.8 68.4 %collective-permute-start.2 = (bf16[1,8,1,32,2048]{4,3,1,2,0:T(8,128)(2,1)S(1)}, bf16[1,8,1,32,2048]{4,3,1,2,0:T(8,128)(2,1)}, u32[]{:S(2)}, u32[]{:S(2)}) collective-permute-start(bf16[1,8,1,32,2048]{4,3,1,2,0:T(8,128)(2,1)S(1)} %collective-permute-done.1), channel_id=1, source_target_pairs={{0,1},{1,2},{2,3},{3,0},{4,5},{5,6},{6,7},{7,4},{8,9},{9,10},{10,1... | collective-permute-start | bytes 3145736 | tf_op jit(solution)/shard_map/ppermute | solution.py:43
  244.4 45.5 %slice-start = ((s8[8388608]{0:T(1024)(128)(4,1)}), s8[4194304]{0:T(1024)(128)(4,1)S(1)}, s32[]{:S(2)}) async-start(s8[8388608]{0:T(1024)(128)(4,1)} %bitcast.66), calls=%async_computation.3 | async-start | bytes 8388608
  254.2 35.7 %slice-start.1 = ((s8[8388608]{0:T(1024)(128)(4,1)}), s8[4194304]{0:T(1024)(128)(4,1)S(1)}, s32[]{:S(2)}) async-start(s8[8388608]{0:T(1024)(128)(4,1)} %bitcast.66), calls=%async_computation.4 | async-start | bytes 8388608
